TPU v7x, 1024 devices: a whole 8x8x8 slice. The times are simulated.
1024 devices in a mesh: dp: 64 (over x_lo, z, core), tp: 16 (over y, x_hi).
Axes of the slice: x: 8 (x_hi: 2, x_lo: 4; x = x_hi * 4 + x_lo), y: 8, z: 8, core: 2. Of those that a mesh axis runs over, the one named last changes fastest.
Arguments:
- hidden_states: bfloat16 [16384, 3584], P('dp'), may hold values from -21 to 21
- resp_lengths: int32 [8], replicated, may hold values from 1 to 8448, 16384 in all
- w_query: bfloat16 [3584, 2048], P('dp', 'tp'), may hold values from -0.25 to 0.25
- w_keyval: bfloat16 [3584, 1024], P('dp', 'tp'), may hold values from -0.09375 to 0.09375
- w_out: bfloat16 [2048, 3584], P('tp', 'dp'), may hold values from -0.125 to 0.125
Outputs:
- attended: bfloat16 [16384, 3584], P('dp', 'tp')
Inputs may be any that keep to these rules, and one draw needn't show every extreme that they name: `resp_lengths`: the 8 lengths sum to 16384; the longest is exactly 8448.
All inputs are finite; a program needn't handle non-finite values.
Results may differ from a plain program's by a relative error of at most 0.015.
The roundings to bfloat16 on the way count: a program that leaves them out, or rounds other values in their place, can miss the bound.
Values may be sent and summed in bfloat16 or wider, within the bound.
A program may use at most 64 MiB of HBM per device.

v0:
```python
import jax
import jax.numpy as jnp
from jax import lax
from jax.sharding import Mesh
from jax.sharding import PartitionSpec as P

HD = 128
DP = ("dp_0", "dp_1", "dp_2")
TP = ("tp_0", "tp_1")


def side_by_side(arrays, axis, dim, along):
    both = jnp.concatenate(arrays, axis=along)
    filled, at, outs = (lax.all_gather(both, axis, axis=dim, tiled=True), 0, [])
    for a in arrays:
        outs.append(lax.slice_in_dim(filled, at, at + a.shape[along], axis=along))
        at += a.shape[along]
    return tuple(outs)


def copy_for_each(value, axis):
    devices = lax.axis_size(axis)
    return lax.all_to_all(
        jnp.broadcast_to(value[None], (devices, *value.shape)), axis, 0, 0, tiled=True
    )


def in_order(tiles, dim):
    shape = list(tiles.shape[1:])
    shape[dim] *= tiles.shape[0]
    return jnp.moveaxis(tiles, 0, dim).reshape(shape)


def gather_directly(value, axis, dim):
    tiles = copy_for_each(value, axis)
    return in_order(tiles, dim)


def gather_in_order(value, axes, order):
    tiles = value[None]
    for k in order:
        tiles = lax.all_gather(tiles, axes[k], axis=0, tiled=True)
    carried = [lax.axis_size(axes[k]) for k in reversed(order)]
    tiles = tiles.reshape(*carried, *value.shape)
    turned = sorted(range(len(order)), key=lambda place: order[len(order) - 1 - place])
    return tiles.transpose(*turned, *range(len(order), tiles.ndim)).reshape(-1, *value.shape)


def whole_of(value, axes, order, dim):
    return in_order(gather_in_order(value, axes, order), dim)


def scatter_axes(value, axes, dim):
    for axis in axes:
        value = lax.psum_scatter(value, axis, scatter_dimension=dim, tiled=True)
    return value


def segment_of(position, resp_ends):
    return jnp.sum(
        (position[:, None] >= resp_ends[None, :]).astype(jnp.int32), axis=1, dtype=jnp.int32
    )


def body(hidden_states, resp_lengths, w_query, w_keyval, w_out):
    token_rows = hidden_states.shape[0]
    head_scale = HD ** (-0.5)
    pieces = side_by_side((w_query, w_keyval), DP, 0, 1)
    query_sum = jnp.dot(hidden_states, pieces[0], preferred_element_type=jnp.float32)
    keyval_sum = jnp.dot(hidden_states, pieces[1], preferred_element_type=jnp.float32)
    query = (query_sum * head_scale).astype(jnp.bfloat16)
    keyval = gather_directly(keyval_sum.astype(jnp.bfloat16), TP, 1)
    kv_count = keyval.shape[1] // (2 * HD)
    per_group = lax.axis_size(TP) // kv_count
    kv_head = lax.axis_index(TP) // per_group
    key_head = lax.dynamic_slice_in_dim(keyval, kv_head * HD, HD, 1)
    value_head = lax.dynamic_slice_in_dim(keyval, (kv_count + kv_head) * HD, HD, 1)
    head_pair = jnp.concatenate([key_head, value_head], axis=1)
    resp_ends = jnp.cumsum(resp_lengths, dtype=jnp.int32)
    own_begin = lax.axis_index(DP) * token_rows
    query_pos = own_begin + jnp.arange(token_rows, dtype=jnp.int32)
    query_seg = segment_of(query_pos, resp_ends)
    pieces = whole_of(head_pair, DP, (0, 1, 2), 0)
    largest = jnp.full((token_rows,), -1e30, jnp.float32)
    height = pieces.shape[0]
    key_pos = jnp.arange(height, dtype=jnp.int32)
    key_seg = segment_of(key_pos, resp_ends)
    scores = jnp.dot(query, pieces[:, :HD].T, preferred_element_type=jnp.float32)
    allowed = (
        (query_seg[:, None] == key_seg[None, :])
        & (key_pos[None, :] <= query_pos[:, None])
        & (key_pos[None, :] >= 0)
    )
    newest = jnp.maximum(largest, jnp.max(jnp.where(allowed, scores, jnp.float32(-1e30)), axis=1))
    expw = jnp.where(allowed, jnp.exp(scores - newest[:, None]), jnp.float32(0.0))
    denom = jnp.sum(expw, axis=1)
    numer = jnp.dot(expw.astype(jnp.bfloat16), pieces[:, HD:], preferred_element_type=jnp.float32)
    heads_out = (numer / denom[:, None]).astype(jnp.bfloat16)
    terms = jnp.dot(heads_out, gather_directly(w_out, DP, 1), preferred_element_type=jnp.float32)
    summed = scatter_axes(terms.astype(jnp.bfloat16), TP, 1).astype(jnp.float32)
    return summed.astype(jnp.bfloat16)


def solution(mesh):
    finer = Mesh(mesh.devices.reshape(4, 8, 2, 8, 2), ("dp_0", "dp_1", "dp_2", "tp_0", "tp_1"))
    placed = (P(DP, None), P(), P(DP, TP), P(DP, TP), P(TP, DP))
    return jax.shard_map(body, mesh=finer, in_specs=placed, out_specs=P(DP, TP), check_vma=False)
```

profile of v0, /device:TPU:14, one launch (start us, length us, event | category | flops | bytes accessed | tf_op | source)
XLA Modules:
  0.0 404.0 jit_solution(8752023980756711703)
XLA Ops:
  6.5 0.0 copy-start
  6.5 0.0 copy-start.1
  6.5 0.0 copy-start.2
  6.5 0.0 all-gather.5.cloned.1.call-start
  6.5 1.5 pad_maximum_fusion.1
  8.0 0.0 all-gather.5.cloned.1.call-update
  8.0 135.1 %all-gather.5.cloned.1.call-done = bf16[3584,192]{1,0:T(8,128)(2,1)} async-done(((bf16[56,192]{1,0:T(8,128)(2,1)}), bf16[3584,192]{1,0:T(8,128)(2,1)}) %all-gather.5.cloned.1.call-update) | async-done | bytes 1376272 | tf_op jit(solution)/shard_map/all_gather | solution.py:14
  143.1 0.0 copy-done
  143.1 1.9 fusion.9
  145.0 0.8 broadcast_in_dim.14
  145.8 12.2 %all-to-all-start = ((bf16[16,256,64]{1,2,0:T(8,128)(2,1)}), bf16[16,256,64]{1,2,0:T(8,128)(2,1)S(1)}, u32[]{:S(2)}, u32[]{:S(2)}) async-start(bf16[16,256,64]{1,2,0:T(8,128)(2,1)} %broadcast_in_dim.14), calls=%async_computation | async-start | bytes 1048576 | tf_op jit(solution)/shard_map/all_to_all | solution.py:23
  158.0 0.0 all-gather.7.cloned.1.call-start
  158.1 16.8 %all-to-all-done = bf16[16,256,64]{1,2,0:T(8,128)(2,1)S(1)} async-done(((bf16[16,256,64]{1,2,0:T(8,128)(2,1)}), bf16[16,256,64]{1,2,0:T(8,128)(2,1)S(1)}, u32[]{:S(2)}, u32[]{:S(2)}) %all-to-all-start) | async-done | bytes 524320 | tf_op jit(solution)/shard_map/all_to_all | solution.py:23
  175.0 16.2 %all-gather = bf16[1024,256]{0,1:T(8,128)(2,1)S(1)} all-gather(bf16[256,256]{0,1:T(8,128)(2,1)S(1)} %pad_maximum_fusion), channel_id=2, replica_groups=mesh['dp_0'=4,'dp_1'=8,'dp_2'=2,'tp_0'=8,'tp_1'=2] {'dp_0'}, dimensions={0}, use_global_device_ids=true | all-gather | bytes 655360 | tf_op jit(solution)/shard_map/all_gather | solution.py:42
  191.1 1.0 copy.14
  192.1 0.0 all-gather.7.cloned.1.call-update
  192.1 0.0 all-gather.9.cloned.1.call-start
  192.2 56.9 %all-gather.7.cloned.1.call-done = bf16[32,256,256]{2,1,0:T(8,128)(2,1)} async-done(((bf16[4,256,256]{2,1,0:T(8,128)(2,1)}), bf16[32,256,256]{2,1,0:T(8,128)(2,1)}) %all-gather.7.cloned.1.call-update) | async-done | bytes 4194320 | tf_op jit(solution)/shard_map/all_gather | solution.py:42
  249.1 0.0 all-gather.9.cloned.1.call-update
  249.1 0.0 copy-done.1
  249.1 1.1 broadcast_in_dim.20
  250.2 7.8 %all-to-all-start.1 = ((bf16[64,128,56]{1,2,0:T(8,128)(2,1)}), bf16[64,128,56]{1,2,0:T(8,128)(2,1)S(1)}, u32[]{:S(2)}, u32[]{:S(2)}) async-start(bf16[64,128,56]{1,2,0:T(8,128)(2,1)} %broadcast_in_dim.20), calls=%async_computation.1 | async-start | bytes 1835008 | tf_op jit(solution)/shard_map/all_to_all | solution.py:23
  258.0 0.2 reduce-scatter.3.cloned.1.call-start
  258.2 0.0 copy-done.2
  258.2 0.2 reduce-window.8
  258.4 0.1 convert_reduce_fusion.1
  258.5 0.3 convert_reduce_fusion
  258.8 21.2 %all-gather.9.cloned.1.call-done = bf16[64,256,256]{2,1,0:T(8,128)(2,1)} async-done(((bf16[32,256,256]{2,1,0:T(8,128)(2,1)}), bf16[64,256,256]{2,1,0:T(8,128)(2,1)}) %all-gather.9.cloned.1.call-update) | async-done | bytes 8388624 | tf_op jit(solution)/shard_map/all_gather | solution.py:42
  280.0 7.6 %copy.13 = bf16[4,8,2,256,256]{4,3,2,1,0:T(8,128)(2,1)} copy(bf16[4,8,2,256,256]{4,3,0,1,2:T(8,128)(2,1)} %bitcast.18) | data formatting | bytes 16777216 | tf_op jit(solution)/shard_map/transpose | solution.py:46
  287.6 12.1 %select_reduce_fusion = (f32[256]{0:T(256)S(1)}, f32[256,16384]{1,0:T(8,128)}) fusion(s32[256]{0:T(256)S(1)} %iota_add_fusion, s32[16384]{0:T(1024)S(1)} %convert_reduce_fusion, s32[256]{0:T(256)S(1)} %convert_reduce_fusion.1, bf16[16384,256]{1,0:T(8,128)(2,1)} %bitcast.19, bf16[256,3584]{1,0:T(8,128)(2,1)S(1)} %copy-done, ...), kind=kOutput, calls=%fused_computation.1 | convolution fusion | flops 1329659648 | bytes 23792640 | tf_op jit(solution)/shard_map/dot_general | solution.py:88
  299.8 8.7 %fusion.1 = f32[256]{0:T(256)S(1)} fusion(f32[256,16384]{1,0:T(8,128)} %get-tuple-element.8, f32[256]{0:T(256)S(1)} %broadcast_maximum_fusion, s32[256]{0:T(256)S(1)} %iota_add_fusion, s32[16384]{0:T(1024)S(1)} %convert_reduce_fusion, s32[256]{0:T(256)S(1)} %convert_reduce_fusion.1), kind=kLoop, calls=%fused_computation.4 | loop fusion | flops 25165568 | bytes 16846848 | tf_op jit(solution)/shard_map/reduce_sum | solution.py:96
  308.4 0.0 all-to-all-done.1
  308.4 13.6 %convolution_convert_fusion = bf16[256,3584]{0,1:T(8,128)(2,1)} fusion(bf16[128,3584]{0,1:T(8,128)(2,1)S(1)} %bitcast.22, bf16[16384,256]{1,0:T(8,128)(2,1)} %bitcast.20, f32[256,16384]{1,0:T(8,128)} %get-tuple-element.8, f32[256]{0:T(256)S(1)} %broadcast_maximum_fusion, s32[256]{0:T(256)S(1)} %iota_add_fusion, s32[16384]{0:T(1024)S(1)} %convert_reduce_fusion, ...), kind=kOutput, calls=%fused_computation.7 | convolution fusion | flops 1334771712 | bytes 23793664 | tf_op jit(solution)/shard_map/dot_general | solution.py:99
  322.0 0.0 reduce-scatter.3.cloned.1.call-update
  322.1 0.0 reduce-scatter.5.cloned.1.call-start
  322.1 49.1 %reduce-scatter.3.cloned.1.call-done = bf16[256,448]{0,1:T(8,128)(2,1)} async-done(((bf16[256,3584]{0,1:T(8,128)(2,1)}), bf16[256,448]{0,1:T(8,128)(2,1)}) %reduce-scatter.3.cloned.1.call-update) | async-done | bytes 229392 | tf_op jit(solution)/shard_map/reduce_scatter | solution.py:55
  371.2 0.0 reduce-scatter.5.cloned.1.call-update
  371.3 26.2 %reduce-scatter.5.cloned.1.call-done = bf16[256,224]{0,1:T(8,128)(2,1)} async-done(((bf16[256,448]{0,1:T(8,128)(2,1)}), bf16[256,224]{0,1:T(8,128)(2,1)}) %reduce-scatter.5.cloned.1.call-update) | async-done | bytes 114704 | tf_op jit(solution)/shard_map/reduce_scatter | solution.py:55
  (4 shorter events, 0.0 us)
Async XLA Ops:
  6.5 136.6 %copy-start = (bf16[256,3584]{1,0:T(8,128)(2,1)S(1)}, bf16[256,3584]{1,0:T(8,128)(2,1)}, u32[]{:S(2)}) copy-start(bf16[256,3584]{1,0:T(8,128)(2,1)} %param.5) | copy-start | bytes 5505028
  6.5 242.6 %copy-start.1 = (bf16[128,56]{0,1:T(8,128)(2,1)S(1)}, bf16[128,56]{0,1:T(8,128)(2,1)}, u32[]{:S(2)}) copy-start(bf16[128,56]{0,1:T(8,128)(2,1)} %param.9) | copy-start | bytes 43012
  6.5 251.7 %copy-start.2 = (s32[8]{0:T(128)S(1)}, s32[8]{0:T(128)}, u32[]{:S(2)}) copy-start(s32[8]{0:T(128)} %param.6) | copy-start | bytes 100
  6.5 136.6 %all-gather.5.cloned.1.call-start = ((), (), s32[]{:S(2)}) async-start(), calls=%async_computation.4 | async-start | bytes 1863680 | tf_op jit(solution)/shard_map/all_gather | solution.py:14
  145.8 29.1 %all-to-all-start = ((bf16[16,256,64]{1,2,0:T(8,128)(2,1)}), bf16[16,256,64]{1,2,0:T(8,128)(2,1)S(1)}, u32[]{:S(2)}, u32[]{:S(2)}) async-start(bf16[16,256,64]{1,2,0:T(8,128)(2,1)} %broadcast_in_dim.14), calls=%async_computation | async-start | bytes 1048576 | tf_op jit(solution)/shard_map/all_to_all | solution.py:23
  158.0 91.1 %all-gather.7.cloned.1.call-start = ((), (), s32[]{:S(2)}) async-start(), calls=%async_computation.5 | async-start | bytes 4718592 | tf_op jit(solution)/shard_map/all_gather | solution.py:42
  192.1 87.9 %all-gather.9.cloned.1.call-start = ((), (), s32[]{:S(2)}) async-start(), calls=%async_computation.6 | async-start | bytes 12582912 | tf_op jit(solution)/shard_map/all_gather | solution.py:42
  250.2 58.2 %all-to-all-start.1 = ((bf16[64,128,56]{1,2,0:T(8,128)(2,1)}), bf16[64,128,56]{1,2,0:T(8,128)(2,1)S(1)}, u32[]{:S(2)}, u32[]{:S(2)}) async-start(bf16[64,128,56]{1,2,0:T(8,128)(2,1)} %broadcast_in_dim.20), calls=%async_computation.1 | async-start | bytes 1835008 | tf_op jit(solution)/shard_map/all_to_all | solution.py:23
  258.0 113.2 %reduce-scatter.3.cloned.1.call-start = ((), (), s32[]{:S(2)}) async-start(), calls=%async_computation.7 | async-start | bytes 2064384 | tf_op jit(solution)/shard_map/reduce_scatter | solution.py:55
  322.1 75.4 %reduce-scatter.5.cloned.1.call-start = ((), (), s32[]{:S(2)}) async-start(), calls=%async_computation.8 | async-start | bytes 344064 | tf_op jit(solution)/shard_map/reduce_scatter | solution.py:55
Sparse Core Ops, SparseCore 0:
  10.1 132.9 all-gather.4
  192.3 56.7 all-gather.6
  251.8 28.1 all-gather.8
  322.2 49.0 reduce-scatter.2
  374.4 23.0 reduce-scatter.4
where the time goes:
time: 410 us; the launch traced here: 404 us
  waiting for transfers between devices  305 us (74%)
  matrix products  27.6 us (7%)
  starting transfers between devices  20.3 us (5%)
  blocking collectives  16.2 us (4%)
  between operations  13.2 us (3%)
  other arithmetic  10.8 us (3%)
  local copies, waits for them, and re-layouts  10.5 us (3%)
    all_gather x1, waiting for transfers between devices, side_by_side(): filled, at, outs = (lax.all_gather(both, axis, axis=dim, tiled=True), 0, [])  135 us
    all_gather x2, waiting for transfers between devices, gather_in_order(): tiles = lax.all_gather(tiles, axes[k], axis=0, tiled=True)  78.1 us
    reduce_scatter x2, waiting for transfers between devices, scatter_axes(): value = lax.psum_scatter(value, axis, scatter_dimension=dim, tiled=True)  75.4 us
    all_to_all x2, starting transfers between devices, copy_for_each(): lax.all_to_all(jnp.broadcast_to(value[None], (devices, *value.shape)), ax...  20 us
    all_to_all x2, waiting for transfers between devices, copy_for_each(): lax.all_to_all(jnp.broadcast_to(value[None], (devices, *value.shape)), ax...  16.8 us
    all_gather x1, blocking collectives, gather_in_order(): tiles = lax.all_gather(tiles, axes[k], axis=0, tiled=True)  16.2 us
    dot_general x1, matrix products, body(): jnp.dot(heads_out, gather_directly(w_out, DP, 1), preferred_element_type=...  13.6 us
    dot_general x1, matrix products, body(): jnp.dot(query, pieces[:, :HD].T, preferred_element_type=jnp.float32)  12.1 us
  transfers between devices with their start and end apart: 7, of which 6 were waited for; matrix products, arithmetic and copies ran while one was open for 7% of the time, Pallas kernels for 0%

commit v1 on v0

v1 whole, which is shorter than its diff:
```python
import functools

import jax
import jax.numpy as jnp
from jax import lax
from jax.experimental import pallas as pl
from jax.experimental.pallas import tpu as pltpu
from jax.sharding import Mesh
from jax.sharding import PartitionSpec as P

HD = 128
DP = ("dp_0", "dp_1", "dp_2")
TP = ("tp_0", "tp_1")
MESH = pl.DeviceIdType.MESH
F32, BF16 = jnp.float32, jnp.bfloat16
NX, NZ, NC, NY, NH = 4, 8, 2, 8, 2
LOW = -1e30


def wrap(a, n):
    return lax.rem(a + 2 * n, n)


class Book:
    def __init__(self, send, recv):
        self.send, self.recv, self.n_send, self.n_recv, self.open = send, recv, 0, 0, []

    def slot(self, count=1):
        at = self.n_recv
        self.n_recv += count
        return at

    def start(self, src, dst, recv_at, device, pred=None):
        at = self.n_send
        self.n_send += 1
        copy = pltpu.make_async_remote_copy(
            src_ref=src, dst_ref=dst, send_sem=self.send.at[at], recv_sem=self.recv.at[recv_at],
            device_id=device, device_id_type=MESH)
        self.open.append((copy, pred))
        if pred is None:
            copy.start()
        else:
            pl.when(pred)(copy.start)

    def wait(self, dst, recv_at, pred=None):
        copy = pltpu.make_async_remote_copy(
            src_ref=dst, dst_ref=dst, send_sem=self.send.at[0], recv_sem=self.recv.at[recv_at],
            device_id={"dp_2": 1 - lax.axis_index("dp_2")}, device_id_type=MESH)
        if pred is None:
            copy.wait_recv()
        else:
            pl.when(pred)(copy.wait_recv)

    def finish(self):
        for copy, pred in self.open:
            if pred is None:
                copy.wait_send()
            else:
                pl.when(pred)(copy.wait_send)


class Plane:
    def __init__(self, book, buf, pos, up, down):
        self.book, self.buf, self.up, self.down = book, buf, up, down
        self.x, self.z, self.c = pos
        self.rx, self.rup, self.rdown = book.slot(3), book.slot(up), book.slot(down)
        self.rcore = book.slot(up + down + 1)

    def core(self, at, zz):
        ref = self.buf.at[self.c, zz]
        self.book.start(ref, ref, self.rcore + at, {"dp_2": 1 - self.c})

    def x_send(self):
        ref = self.buf.at[self.c, self.z, self.x]
        for d in (1, 2, 3):
            self.book.start(ref, ref, self.rx + d - 1, {"dp_0": wrap(self.x + d, NX)})

    def hop(self, k, step):
        zz = wrap(self.z - step * (k - 1), NZ)
        ref = self.buf.at[self.c, zz]
        base = self.rup if step == 1 else self.rdown
        self.book.start(ref, ref, base + k - 1, {"dp_1": wrap(self.z + step, NZ)})

    def x_wait(self):
        for d in (1, 2, 3):
            self.book.wait(self.buf.at[self.c, self.z, wrap(self.x - d, NX)], self.rx + d - 1)
        self.hop(1, 1)
        self.hop(1, -1)
        self.core(0, self.z)

    def step(self, k):
        for step, last, base, at in ((1, self.up, self.rup, 0), (-1, self.down, self.rdown, self.up)):
            if k <= last:
                zz = wrap(self.z - step * k, NZ)
                self.book.wait(self.buf.at[self.c, zz], base + k - 1)
                if k < last:
                    self.hop(k + 1, step)
                self.core(at + k, zz)

    def core_wait(self):
        for k in range(self.up + 1):
            self.book.wait(self.buf.at[1 - self.c, wrap(self.z - k, NZ)], self.rcore + k)
        for k in range(1, self.down + 1):
            self.book.wait(self.buf.at[1 - self.c, wrap(self.z + k, NZ)], self.rcore + self.up + k)


def received(step, k, row, z):
    if step == 1:
        if row == 0:
            return z >= k
        if row == 1:
            return None if k > 4 else (z >= 0 if k <= 3 else z < 4)
        if k == 1:
            return z >= 0
        if k == 2:
            return (z <= 1) | (z == 7)
        return z <= 2 if k == 3 else None
    if row == 2:
        return z <= 7 - k
    if row == 1:
        return z >= 0 if k <= 3 else z >= 4
    if k == 1:
        return (z == 7) | (z <= 1)
    if k == 2:
        return (z >= 6) | (z == 0)
    return z >= 5 if k == 3 else None


def needed(step, k, row, z):
    if row == 1:
        return received(step, k, row, z)
    if row == 0:
        return (z >= k) if step == 1 else (None if k > 3 else z + k >= 8)
    if step == -1:
        return z <= 7 - k
    if k == 1:
        return z >= 0
    return z < k if k <= 3 else None


def kernel(hid, qstart, wq_in, wx_in, wo_in, out,
           g_q, g_x, g_o, land, w_q, w_x, w_t, qq, made, kv, acc, stat, o_in, stat_in, heads, total,
           send_sem, recv_sem):
    x, z, c = (lax.axis_index(a) for a in DP)
    y, h = (lax.axis_index(a) for a in TP)
    p = lax.rem(y, 2)
    y2 = y + 1 - 2 * p
    book = Book(send_sem, recv_sem)

    y_to = lax.rem(2 * y, NY) + lax.div(y, 4)
    y_from = lax.div(y, 2) + 4 * p
    o_to = (2 * h + lax.rem(z, 2), y, 2 * x + lax.div(z, 4), lax.rem(lax.div(z, 2), 2))
    o_from = (lax.div(y, 2), 4 * p + 2 * h + lax.rem(x, 2), z, lax.div(x, 2))

    def xzyh(t):
        return {"dp_0": t[0], "dp_1": t[1], "tp_0": t[2], "tp_1": t[3]}

    o_self = (o_to[0] == x) & (o_to[1] == z) & (o_to[2] == y) & (o_to[3] == h)
    barrier = pltpu.get_barrier_semaphore()

    def greet(device, own=None):
        def remote():
            pl.semaphore_signal(barrier, inc=1, device_id=device, device_id_type=MESH)

        if own is None:
            remote()
        else:
            pl.when(jnp.logical_not(own))(remote)

    greet(xzyh(o_to), o_self)
    greet(xzyh(o_from), o_self)
    for j in (0, 1):
        greet({"tp_0": y_to, "tp_1": j}, (y_to == y) & (h == j))
        greet({"tp_0": y_from, "tp_1": j}, (y_from == y) & (h == j))
    greet({"dp_0": 3 - x, "dp_1": 7 - z})
    greet({"tp_1": 1 - h})
    for d in (1, 2, 3):
        greet({"dp_0": wrap(x + d, NX)})
    for d in (1, -1):
        greet({"dp_1": wrap(z + d, NZ)})
        greet({"tp_0": wrap(y + d, NY)})
    greet({"tp_0": y2, "dp_2": 1 - c})
    greet({"dp_2": 1 - c})

    g_q[c, z, x] = wq_in[...]
    acc[...] = jnp.zeros_like(acc)
    stat[:, 0] = jnp.full((2, 8, 256), LOW, F32)
    stat[:, 1] = jnp.zeros((2, 8, 256), F32)
    pl.semaphore_wait(barrier, 17 - jnp.where(o_self, 2, 0) - jnp.where(y_to == y, 2, 0))

    r_land, r_o = book.slot(2), book.slot(1)
    pos = (x, z, c)
    gq = Plane(book, g_q, pos, 4, 3)
    gx = Plane(book, g_x, pos, 3, 4)
    go = Plane(book, g_o, pos, 4, 3)

    gq.x_send()

    def to_or_own(src, dst, recv_at, device, own):
        book.start(src, dst, recv_at, device, jnp.logical_not(own))

        @pl.when(own)
        def _():
            pltpu.make_async_copy(src, dst, recv_sem.at[recv_at]).start()

    for j in (0, 1):
        own = (y_to == y) & (h == j)
        for hh in (0, 1):
            here = h == hh
            book.start(wx_in, land.at[hh], r_land + hh, {"tp_0": y_to, "tp_1": j}, here & jnp.logical_not(own))

            @pl.when(here & own)
            def _():
                pltpu.make_async_copy(wx_in, land.at[hh], recv_sem.at[r_land + hh]).start()
    o_slot = g_o.at[c, y, 2 * h + lax.rem(z, 2)]
    to_or_own(wo_in, o_slot, r_o, xzyh(o_to), o_self)

    gq.x_wait()
    book.wait(land.at[0], r_land)
    book.wait(land.at[1], r_land + 1)
    lane = lax.broadcasted_iota(jnp.int32, (56, HD), 1)
    g_x[c, z, x] = jnp.where(lane < 64, land[0].astype(F32), land[1].astype(F32)).astype(BF16)
    gx.x_send()
    gq.step(1)
    gx.x_wait()
    gq.step(2)
    gx.step(1)
    gq.step(3)
    gx.step(2)
    gq.step(4)
    gx.step(3)
    gx.step(4)
    book.wait(g_o.at[c, z, x], r_o)
    go.x_send()

    def assemble(g, w):
        def one(i, carry):
            xx, zz = lax.div(i, NZ), lax.rem(i, NZ)
            both = jnp.concatenate([g[0, zz, xx].astype(F32), g[1, zz, xx].astype(F32)], axis=0)
            w[i] = both.astype(BF16)
            return carry

        lax.fori_loop(0, NX * NZ, one, 0)

    r_q = book.slot(1)
    gq.core_wait()
    assemble(g_q, w_q)
    q_sum = jnp.dot(hid[...], w_q[...].reshape(3584, HD), preferred_element_type=F32)
    qq[p] = (q_sum * (HD ** -0.5)).astype(BF16)
    book.start(qq.at[p], qq.at[p], r_q, {"tp_0": y2})
    gx.core_wait()
    assemble(g_x, w_x)
    x_sum = jnp.dot(hid[...], w_x[...].reshape(3584, HD), preferred_element_type=F32)

    halves = x_sum.reshape(2, HD, HD)
    turned = jnp.stack([halves[0].T, halves[1].T])
    block = jnp.where(p == 0, halves, turned).astype(BF16)
    moves = c != p
    mine = kv.at[c, z, 0]

    @pl.when(moves)
    def _():
        made[...] = block

    @pl.when(jnp.logical_not(moves))
    def _():
        kv[c, z, 0] = block

    r_pair = book.slot(1)
    book.start(made, kv.at[p, z, 0], r_pair, {"tp_0": y2, "dp_2": 1 - c}, moves)
    book.wait(mine, r_pair, moves)

    n_steps = 4
    r_xk = book.slot(2)
    r_ring = {(s, k, r): book.slot(1) for s in (1, -1) for k in range(1, 5) for r in range(3)}
    r_cx = book.slot(3)
    r_cring = {(s, k, r): book.slot(1) for s in (1, -1) for k in range(1, 5) for r in range(3)}
    r_far, r_cfar = book.slot(1), book.slot(1)

    far_from = (x == 0) & (z == 7) & (p == 1)
    far_to = (x == 3) & (z == 0) & (p == 1)
    far = kv.at[c, NZ, 0]
    for d in (1, 2):
        book.start(mine, kv.at[c, z, d], r_xk + d - 1, {"dp_0": wrap(x + d, NX)}, x + d <= 3)
    book.start(mine, far, r_far, {"dp_0": 3 - x, "dp_1": 7 - z}, far_from)

    def ring(k, rows, step):
        for r in rows:
            to = wrap(z + step, NZ)
            pred = received(step, k, r, to)
            if pred is not None:
                ref = kv.at[c, wrap(z - step * (k - 1), NZ), r]
                book.start(ref, ref, r_ring[step, k, r], {"dp_1": to}, pred & (x >= r))

    def to_core(ref, at, pred):
        book.start(ref, ref, at, {"dp_2": 1 - c}, pred)

    for s in (1, -1):
        ring(1, (0,), s)
    to_core(mine, r_cx, None)
    for d in (1, 2):
        book.wait(kv.at[c, z, d], r_xk + d - 1, x >= d)
        for s in (1, -1):
            ring(1, (d,), s)
        to_core(kv.at[c, z, d], r_cx + d, x >= d)

    book.wait(qq.at[1 - p], r_q)
    q_pos = (2 * (x * NZ + z) + c) * 256 + lax.broadcasted_iota(jnp.int32, (1, 256), 1)
    q_low = qstart[...]

    def attend(zz, row, chunk):
        keys = kv[0, zz, row].reshape(256, HD)
        k_pos = (2 * chunk + p) * 256 + lax.broadcasted_iota(jnp.int32, (256, 256), 0)
        allowed = (k_pos >= q_low) & (k_pos <= q_pos)
        for hd in (0, 1):
            scores = lax.dot_general(keys, qq[hd], (((1,), (1,)), ((), ())), preferred_element_type=F32)
            scores = jnp.where(allowed, scores, LOW)
            old = stat[hd, 0, 0:1]
            new = jnp.maximum(old, jnp.max(scores, axis=0, keepdims=True))
            expw = jnp.where(allowed, jnp.exp(scores - new), 0.0)
            scale = jnp.exp(old - new)
            stat[hd, 1] = stat[hd, 1] * scale + jnp.sum(expw, axis=0, keepdims=True)
            stat[hd, 0] = jnp.broadcast_to(new, (8, 256))
            probs = expw.astype(BF16)
            numer = jnp.dot(kv[1, zz, row, 0], probs[:HD], preferred_element_type=F32)
            numer = numer + jnp.dot(kv[1, zz, row, 1], probs[HD:], preferred_element_type=F32)
            acc[hd] = acc[hd] * scale + numer

    def attend_some(preds, place):
        def one(i, carry):
            on = i < 0
            for n, pred in enumerate(preds):
                if pred is not None:
                    on = on | ((i == n) & pred)

            @pl.when(on)
            def _():
                zz, row = place(i)
                attend(zz, row, (x - row) * NZ + zz)

            return carry

        lax.fori_loop(0, len(preds), one, 0)

    def attend_own():
        for d in (0, 1, 2):
            book.wait(kv.at[1 - c, z, d], r_cx + d, None if d == 0 else x >= d)
        attend_some([x >= 0, x >= 1, x >= 2], lambda i: (z, i))

    def attend_step(k):
        preds = []
        for s in (1, -1):
            for r in range(3):
                need = needed(s, k, r, z)
                if need is not None:
                    need = need & (x >= r)
                    book.wait(kv.at[1 - c, wrap(z - s * k, NZ), r], r_cring[s, k, r], need)
                preds.append(need)
        attend_some(preds, lambda i: (wrap(z - k + 2 * k * lax.div(i, 3), NZ), lax.rem(i, 3)))

    for k in range(1, n_steps + 1):
        for s in (1, -1):
            for r in range(3):
                got = received(s, k, r, z)
                if got is None:
                    continue
                ref = kv.at[c, wrap(z - s * k, NZ), r]
                book.wait(ref, r_ring[s, k, r], got & (x >= r))
                if k < n_steps:
                    ring(k + 1, (r,), s)
                to_core(ref, r_cring[s, k, r], needed(s, k, r, z) & (x >= r))
        if k == 3:
            go.x_wait()
        if k == 4:
            go.step(1)
        if k == 1:
            book.wait(far, r_far, far_to)
            to_core(far, r_cfar, far_to)
            attend_own()
        else:
            attend_step(k - 1)
    go.step(2)
    attend_step(4)
    book.wait(kv.at[1 - c, NZ, 0], r_cfar, far_to)

    @pl.when(far_to)
    def _():
        attend(NZ, 0, 7)

    r_acc, r_stat = book.slot(1), book.slot(1)
    book.start(stat.at[1 - p], stat_in, r_stat, {"tp_0": y2})
    book.start(acc.at[1 - p], o_in, r_acc, {"tp_0": y2})
    go.step(3)
    book.wait(stat_in, r_stat)
    book.wait(o_in, r_acc)
    m_a, m_b = stat[p, 0, 0:1], stat_in[0, 0:1]
    top = jnp.maximum(m_a, m_b)
    e_a, e_b = jnp.exp(m_a - top), jnp.exp(m_b - top)
    denom = stat[p, 1, 0:1] * e_a + stat_in[1, 0:1] * e_b
    heads[y, h] = ((acc[p] * e_a + o_in[...] * e_b) / denom).astype(BF16)

    r_h = book.slot(1)
    r_head = [{(s, k): book.slot(1) for s in (1, -1) for k in range(1, 5)} for _ in range(2)]
    last = ({1: 4, -1: 3}, {1: 3, -1: 4})
    own_heads = heads.at[y, h]
    book.start(own_heads, own_heads, r_h, {"tp_1": 1 - h})

    def head_hop(which, k, s):
        ref = heads.at[wrap(y - s * (k - 1), NY), h if which == 0 else 1 - h]
        book.start(ref, ref, r_head[which][s, k], {"tp_0": wrap(y + s, NY)})

    def head_step(which, k):
        for s in (1, -1):
            if k <= last[which][s]:
                book.wait(heads.at[wrap(y - s * k, NY), h if which == 0 else 1 - h], r_head[which][s, k])
                if k < last[which][s]:
                    head_hop(which, k + 1, s)

    for s in (1, -1):
        head_hop(0, 1, s)
    go.step(4)
    head_step(0, 1)
    go.core_wait()

    def weights(t, carry):
        yy, hh = lax.div(t, 2), lax.rem(t, 2)
        parts = [g_o[cc, yy, 2 * hh + b].astype(F32) for b in (0, 1) for cc in (0, 1)]
        w_t[t] = jnp.concatenate(parts, axis=0).astype(BF16)
        return carry

    lax.fori_loop(0, NY * NH, weights, 0)
    book.wait(heads.at[y, 1 - h], r_h)
    for s in (1, -1):
        head_hop(1, 1, s)
    for k in (1, 2, 3):
        head_step(0, k + 1)
        head_step(1, k)
    head_step(1, 4)

    total[...] = jnp.zeros_like(total)

    def group(t, carry):
        yy, hh = lax.div(t, 2), lax.rem(t, 2)
        term = jnp.dot(w_t[t], heads[yy, hh], preferred_element_type=F32).astype(BF16)
        total[0:224] = total[0:224] + term.astype(F32)
        return carry

    lax.fori_loop(0, NY * NH, group, 0)
    out[...] = total[...].T[:, :224].astype(BF16)
    book.finish()


def body(hidden_states, resp_lengths, w_query, w_keyval, w_out):
    rows = hidden_states.shape[0]
    ends = jnp.cumsum(resp_lengths, dtype=jnp.int32)
    q_pos = lax.axis_index(DP) * rows + jnp.arange(rows, dtype=jnp.int32)
    begun = jnp.where(q_pos[None, :] >= ends[:, None], ends[:, None], 0)
    q_start = jnp.max(begun, axis=0)[None, :]
    wx = jnp.concatenate([w_keyval, w_keyval], axis=1)
    wo = w_out.T
    vmem = pl.BlockSpec(memory_space=pltpu.VMEM)
    return pl.pallas_call(
        kernel,
        out_shape=jax.ShapeDtypeStruct((rows, 224), BF16),
        in_specs=[vmem] * 5,
        out_specs=vmem,
        scratch_shapes=[
            pltpu.VMEM((NC, NZ, NX, 56, HD), BF16),
            pltpu.VMEM((NC, NZ, NX, 56, HD), BF16),
            pltpu.VMEM((NC, NZ, NX, 56, HD), BF16),
            pltpu.VMEM((2, 56, HD), BF16),
            pltpu.VMEM((NX * NZ, 112, HD), BF16),
            pltpu.VMEM((NX * NZ, 112, HD), BF16),
            pltpu.VMEM((16, 224, HD), BF16),
            pltpu.VMEM((2, 256, HD), BF16),
            pltpu.VMEM((2, HD, HD), BF16),
            pltpu.VMEM((2, NZ + 1, 3, 2, HD, HD), BF16),
            pltpu.VMEM((2, HD, 256), F32),
            pltpu.VMEM((2, 2, 8, 256), F32),
            pltpu.VMEM((HD, 256), F32),
            pltpu.VMEM((2, 8, 256), F32),
            pltpu.VMEM((NY, NH, HD, 256), BF16),
            pltpu.VMEM((256, 256), F32),
            pltpu.SemaphoreType.DMA((160,)),
            pltpu.SemaphoreType.DMA((160,)),
        ],
        compiler_params=pltpu.CompilerParams(
            collective_id=0, has_side_effects=True, vmem_limit_bytes=48 * 1024 * 1024),
        name="layer",
    )(hidden_states, q_start, w_query, wx, wo)


def solution(mesh):
    finer = Mesh(mesh.devices.reshape(4, 8, 2, 8, 2), (*DP, *TP))
    placed = (P(DP, None), P(), P(DP, TP), P(DP, TP), P(TP, DP))
    return jax.shard_map(body, mesh=finer, in_specs=placed, out_specs=P(DP, TP), check_vma=False)
```

time: 410 us -> 117 us (0.29); the launches traced: 404 us -> 116 us
  waiting for transfers between devices: 305 us -> 0 us
  Pallas kernels: 0 us -> 110 us
  matrix products: 27.6 us -> 0 us
  starting transfers between devices: 20.3 us -> 0 us
  blocking collectives: 16.2 us -> 0 us
  between operations: 13.2 us -> 0.01 us
  other arithmetic: 10.8 us -> 1.78 us
  local copies, waits for them, and re-layouts: 10.5 us -> 3.67 us
    all_gather x3 -> x0, waiting for transfers between devices: 213 us -> none  [the longest x1 135 us: side_by_side(): filled, at, outs = (lax.all_gather(both, axis, axis=dim, tiled=True), 0, [])]
    pallas_call x0 -> x1, Pallas kernels: none -> 110 us  [body(): pl.pallas_call(kernel, out_shape=jax.ShapeDtypeStruct((rows, 224), BF16),...]
    reduce_scatter x2 -> x0, waiting for transfers between devices: 75.4 us -> none  [scatter_axes(): value = lax.psum_scatter(value, axis, scatter_dimension=dim, tiled=True)]
    dot_general x3 -> x0, matrix products: 27.6 us -> none  [the longest x1 13.6 us: body(): jnp.dot(heads_out, gather_directly(w_out, DP, 1), preferred_element_type=...]
    all_to_all x2 -> x0, starting transfers between devices: 20 us -> none  [copy_for_each(): lax.all_to_all(jnp.broadcast_to(value[None], (devices, *value.shape)), ax...]
    all_to_all x2 -> x0, waiting for transfers between devices: 16.8 us -> none  [copy_for_each(): lax.all_to_all(jnp.broadcast_to(value[None], (devices, *value.shape)), ax...]
    all_gather x1 -> x0, blocking collectives: 16.2 us -> none  [gather_in_order(): tiles = lax.all_gather(tiles, axes[k], axis=0, tiled=True)]
    reduce_sum x3 -> x0, other arithmetic: 9.07 us -> none  [the longest x1 8.68 us: body(): denom = jnp.sum(expw, axis=1)]
  transfers between devices with their start and end apart: 7 -> 0, of which waited for: 6 -> 0; matrix products, arithmetic and copies ran while one was open for 7% -> 0% of each run, Pallas kernels for 0% -> 0%
where the time goes in v1:
time: 117 us; the launch traced here: 116 us
  Pallas kernels  110 us (94%)
  local copies, waits for them, and re-layouts  3.67 us (3%)
  other arithmetic  1.78 us (2%)
    pallas_call x1, Pallas kernels, body(): pl.pallas_call(kernel, out_shape=jax.ShapeDtypeStruct((rows, 224), BF16),...  110 us
    unnamed x6, local copies, waits for them, and re-layouts  2.92 us

profile of v1, /device:TPU:14, one launch (start us, length us, event | category | flops | bytes accessed | tf_op | source)
XLA Modules:
  0.0 115.7 jit_solution(6823957432552730316)
XLA Ops:
  0.0 0.8 reduce-window.8
  0.8 0.1 select_reduce_fusion
  0.9 0.9 pad_maximum_fusion.wx_in
  1.8 0.0 copy-start
  1.8 1.5 %copy-done = bf16[256,3584]{1,0:T(8,128)(2,1)S(1)} copy-done((bf16[256,3584]{1,0:T(8,128)(2,1)S(1)}, bf16[256,3584]{1,0:T(8,128)(2,1)}, u32[]{:S(2)}) %copy-start) | copy-done | bytes 1835032
  3.3 0.0 copy-start.1
  3.3 0.7 copy-done.1
  4.0 0.0 copy-start.2
  4.0 0.7 copy-done.2
  4.7 110.3 %layer.1 = bf16[256,224]{1,0:T(8,128)(2,1)S(1)} custom-call(bf16[256,3584]{1,0:T(8,128)(2,1)S(1)} %copy-done, s32[1,256]{1,0:T(1,128)S(1)} %bitcast.5, bf16[56,128]{1,0:T(8,128)(2,1)S(1)} %copy-done.1, bf16[56,128]{1,0:T(8,128)(2,1)S(1)} %pad_maximum_fusion.wx_in, bf16[56,128]{1,0:T(8,128)(2,1)S(1)} %bitcast.4), custom_call_target="tpu_custom_call" | custom-call | tf_op jit(solution)/shard_map/layer/pallas_call | solution.py:462
  115.0 0.8 copy.7
  (1 shorter events, 0.0 us)
Async XLA Ops:
  1.8 1.5 %copy-start = (bf16[256,3584]{1,0:T(8,128)(2,1)S(1)}, bf16[256,3584]{1,0:T(8,128)(2,1)}, u32[]{:S(2)}) copy-start(bf16[256,3584]{1,0:T(8,128)(2,1)} %hid.1) | copy-start | bytes 5505028
  3.3 0.7 copy-start.1
  4.0 0.7 copy-start.2

commit v2 on v1

v2 whole, which is shorter than its diff:
```python
import functools

import jax
import jax.numpy as jnp
from jax import lax
from jax.experimental import pallas as pl
from jax.experimental.pallas import tpu as pltpu
from jax.sharding import Mesh
from jax.sharding import PartitionSpec as P

HD = 128
DP = ("dp_0", "dp_1", "dp_2")
TP = ("tp_0", "tp_1")
MESH = pl.DeviceIdType.MESH
F32, BF16 = jnp.float32, jnp.bfloat16
NX, NZ, NC, NY, NH = 4, 8, 2, 8, 2
LOW = -1e30


def wrap(a, n):
    return lax.rem(a + 2 * n, n)


class Book:
    def __init__(self, send, recv):
        self.send, self.recv, self.n_recv, self.open = send, recv, 0, []
        self.free = list(range(send.shape[0]))

    def slot(self, count=1):
        at = self.n_recv
        self.n_recv += count
        return at

    def start(self, src, dst, recv_at, device, pred=None):
        if not self.free:
            self.settle()
        at = self.free.pop(0)
        copy = pltpu.make_async_remote_copy(
            src_ref=src, dst_ref=dst, send_sem=self.send.at[at], recv_sem=self.recv.at[recv_at],
            device_id=device, device_id_type=MESH)
        self.open.append((copy, pred, at))
        if pred is None:
            copy.start()
        else:
            pl.when(pred)(copy.start)

    def wait(self, dst, recv_at, pred=None):
        copy = pltpu.make_async_remote_copy(
            src_ref=dst, dst_ref=dst, send_sem=self.send.at[0], recv_sem=self.recv.at[recv_at],
            device_id={"dp_2": 1 - lax.axis_index("dp_2")}, device_id_type=MESH)
        if pred is None:
            copy.wait_recv()
        else:
            pl.when(pred)(copy.wait_recv)

    def settle(self):
        copy, pred, at = self.open.pop(0)
        if pred is None:
            copy.wait_send()
        else:
            pl.when(pred)(copy.wait_send)
        self.free.append(at)

    def finish(self):
        while self.open:
            self.settle()


class Plane:
    def __init__(self, book, buf, pos, up, down, parts, late):
        self.book, self.buf, self.parts = book, buf, parts
        self.x, self.z, self.c = pos
        self.last = {1: up, -1: down}
        self.rx = book.slot()
        self.rz = {(s, k): book.slot(parts) for s in (1, -1) for k in range(1, self.last[s] + 1)}
        self.late, self.rcore = late, book.slot(1 + late)

    def core(self, k, zz):
        ref = self.buf.at[self.c, zz]
        self.book.start(ref, ref, self.rcore + (1 if self.late and k == 4 else 0), {"dp_2": 1 - self.c})

    def x_send(self):
        ref = self.buf.at[self.c, self.z, self.x]
        for d in (1, 2, 3):
            self.book.start(ref, ref, self.rx, {"dp_0": wrap(self.x + d, NX)})

    def slab(self, zz, part):
        size = NX // self.parts
        return self.buf.at[self.c, zz, pl.ds(part * size, size)]

    def hop(self, k, step, part):
        ref = self.slab(wrap(self.z - step * (k - 1), NZ), part)
        self.book.start(ref, ref, self.rz[step, k] + part, {"dp_1": wrap(self.z + step, NZ)})

    def x_wait(self):
        self.book.wait(self.buf.at[self.c, self.z, pl.ds(0, NX - 1)], self.rx)

    def begin(self):
        for part in range(self.parts):
            self.hop(1, 1, part)
            self.hop(1, -1, part)
        self.core(0, self.z)

    def step(self, k):
        steps = [s for s in (1, -1) if k <= self.last[s]]
        for part in range(self.parts):
            for s in steps:
                self.book.wait(self.slab(wrap(self.z - s * k, NZ), part), self.rz[s, k] + part)
                if k < self.last[s]:
                    self.hop(k + 1, s, part)
        for s in steps:
            self.core(k, wrap(self.z - s * k, NZ))

    def core_wait(self, last=False):
        theirs = self.buf.at[1 - self.c]
        if last:
            self.book.wait(theirs.at[0], self.rcore + 1)
        else:
            self.book.wait(theirs.at[pl.ds(0, NZ - 1)] if self.late else theirs, self.rcore)


def received(step, k, row, z):
    if step == 1:
        if row == 0:
            return z >= k
        if row == 1:
            return None if k > 4 else (z >= 0 if k <= 3 else z < 4)
        if k == 1:
            return z >= 0
        if k == 2:
            return (z <= 1) | (z == 7)
        return z <= 2 if k == 3 else None
    if row == 2:
        return z <= 7 - k
    if row == 1:
        return z >= 0 if k <= 3 else z >= 4
    if k == 1:
        return (z == 7) | (z <= 1)
    if k == 2:
        return (z >= 6) | (z == 0)
    return z >= 5 if k == 3 else None


def needed(step, k, row, z):
    if row == 1:
        return received(step, k, row, z)
    if row == 0:
        return (z >= k) if step == 1 else (None if k > 3 else z + k >= 8)
    if step == -1:
        return z <= 7 - k
    if k == 1:
        return z >= 0
    return z < k if k <= 3 else None


def kernel(lengths, hid_in, wq_in, wkv_in, wo_in, out,
           hid, wkv, wx, wo, g_q, g_x, g_o, land, w_q, w_x, w_t, qq, made, kv, acc, stat,
           o_out, o_in, stat_in, heads, total, local_sem, send_sem, recv_sem):
    x, z, c = (lax.axis_index(a) for a in DP)
    y, h = (lax.axis_index(a) for a in TP)
    p = lax.rem(y, 2)
    y2 = y + 1 - 2 * p
    book = Book(send_sem, recv_sem)
    fetches = [pltpu.make_async_copy(src, dst, local_sem.at[n]) for n, (src, dst) in enumerate((
        (wkv_in, wkv), (wq_in, g_q.at[c, z, x]), (wo_in, wo), (hid_in, hid)))]
    for fetch in fetches:
        fetch.start()

    y_to = lax.rem(2 * y, NY) + lax.div(y, 4)
    y_from = lax.div(y, 2) + 4 * p
    o_to = (2 * h + lax.rem(z, 2), y, 2 * x + lax.div(z, 4), lax.rem(lax.div(z, 2), 2))
    o_from = (lax.div(y, 2), 4 * p + 2 * h + lax.rem(x, 2), z, lax.div(x, 2))

    def xzyh(t):
        return {"dp_0": t[0], "dp_1": t[1], "tp_0": t[2], "tp_1": t[3]}

    o_self = (o_to[0] == x) & (o_to[1] == z) & (o_to[2] == y) & (o_to[3] == h)
    barrier = pltpu.get_barrier_semaphore()

    def greet(device, own=None):
        def remote():
            pl.semaphore_signal(barrier, inc=1, device_id=device, device_id_type=MESH)

        if own is None:
            remote()
        else:
            pl.when(jnp.logical_not(own))(remote)

    greet(xzyh(o_to), o_self)
    greet(xzyh(o_from), o_self)
    for d in range(NX):
        for j in (0, 1):
            device = {"dp_0": wrap(x + d, NX), "tp_1": j}
            own = (y_to == y) & (h == j) if d == 0 else None
            greet({**device, "tp_0": y_to}, own)
            greet({**device, "tp_0": y_from}, own)
    greet({"dp_0": 3 - x, "dp_1": 7 - z})
    greet({"tp_1": 1 - h})
    for d in (1, 2, 3):
        greet({"dp_0": wrap(x + d, NX)})
    for d in (1, -1):
        greet({"dp_1": wrap(z + d, NZ)})
        greet({"tp_0": wrap(y + d, NY)})
    for d in range(NX):
        greet({"dp_0": wrap(x + d, NX), "tp_0": y2, "dp_2": 1 - c})
    greet({"dp_2": 1 - c})

    acc[...] = jnp.zeros_like(acc)
    stat[:, 0] = jnp.full((2, 8, 256), LOW, F32)
    stat[:, 1] = jnp.zeros((2, 8, 256), F32)
    fetches[0].wait()
    pair = wkv[...].astype(F32)
    wx[...] = jnp.concatenate([pair, pair], axis=1).astype(BF16)
    fetches[1].wait()
    pl.semaphore_wait(barrier, 32 - jnp.where(o_self, 2, 0) - jnp.where(y_to == y, 2, 0))

    r_land, r_o = book.slot(1), book.slot(1)
    pos = (x, z, c)
    gq = Plane(book, g_q, pos, 4, 3, 2, 0)
    gx = Plane(book, g_x, pos, 3, 4, 2, 1)
    go = Plane(book, g_o, pos, 4, 3, 1, 0)

    def to_or_own(src, dst, recv_at, device, own):
        book.start(src, dst, recv_at, device, jnp.logical_not(own))

        @pl.when(own)
        def _():
            pltpu.make_async_copy(src, dst, recv_sem.at[recv_at]).start()

    for d in range(NX):
        for j in (0, 1):
            device = {"dp_0": wrap(x + d, NX), "tp_0": y_to, "tp_1": j}
            if d == 0:
                to_or_own(wx, land.at[x, h], r_land, device, (y_to == y) & (h == j))
            else:
                book.start(wx, land.at[x, h], r_land, device)
    gq.x_send()

    gq.x_wait()
    gq.begin()
    lane = lax.broadcasted_iota(jnp.int32, (56, HD), 1)
    book.wait(land, r_land)
    for xx in range(NX):
        g_x[c, z, xx] = jnp.where(lane < 64, land[xx, 0].astype(F32), land[xx, 1].astype(F32)).astype(BF16)
    gx.begin()
    fetches[2].wait()
    to_or_own(wo, g_o.at[c, y, 2 * h + lax.rem(z, 2)], r_o, xzyh(o_to), o_self)

    def assemble(g, w, first, count):
        def one(i, carry):
            zz, xx = wrap(z + first + lax.div(i, NX), NZ), lax.rem(i, NX)
            both = jnp.concatenate([g[0, zz, xx].astype(F32), g[1, zz, xx].astype(F32)], axis=0)
            w[xx * NZ + zz] = both.astype(BF16)
            return carry

        lax.fori_loop(0, NX * count, one, 0)

    gq.step(1)
    gx.step(1)
    gq.step(2)
    gx.step(2)
    gq.step(3)
    gx.step(3)
    gq.step(4)
    gq.core_wait()
    assemble(g_q, w_q, 0, NZ)
    fetches[3].wait()
    r_q = book.slot(1)
    q_sum = jnp.dot(hid[...], w_q[...].reshape(3584, HD), preferred_element_type=F32)
    qq[p] = (q_sum * (HD ** -0.5)).astype(BF16)
    gx.core_wait()
    assemble(g_x, w_x, -3, NZ - 1)
    gx.step(4)
    gx.core_wait(True)
    assemble(g_x, w_x, 4, 1)
    x_sum = jnp.dot(hid[...], w_x[...].reshape(3584, HD), preferred_element_type=F32)

    halves = x_sum.reshape(2, HD, HD)
    turned = jnp.stack([halves[0].T, halves[1].T])
    block = jnp.where(p == 0, halves, turned).astype(BF16)
    moves = c != p
    mine = kv.at[c, z, 0]

    @pl.when(moves)
    def _():
        made[...] = block

    @pl.when(jnp.logical_not(moves))
    def _():
        kv[c, z, 0] = block

    r_pair = book.slot(1)
    r_xk = book.slot(2)
    for d in (0, 1, 2):
        fits = x + d <= 3
        book.start(made, kv.at[p, z, d], r_pair if d == 0 else r_xk + d - 1,
                   {"dp_0": wrap(x + d, NX), "tp_0": y2, "dp_2": 1 - c}, moves & fits)
        if d > 0:
            book.start(mine, kv.at[c, z, d], r_xk + d - 1, {"dp_0": wrap(x + d, NX)}, jnp.logical_not(moves) & fits)
    book.start(qq.at[p], qq.at[p], r_q, {"tp_0": y2})
    book.wait(mine, r_pair, moves)

    n_steps = 4
    hops = [(s, k, r) for s in (1, -1) for k in range(1, 5) for r in range(3) if received(s, k, r, z) is not None]
    r_ring = {hop: book.slot(2) for hop in hops}
    r_cx = book.slot(3)
    r_cring = {hop: book.slot(1) for hop in hops}
    r_far, r_cfar = book.slot(1), book.slot(1)

    far_from = (x == 0) & (z == 7) & (p == 1)
    far_to = (x == 3) & (z == 0) & (p == 1)
    far = kv.at[c, NZ, 0]
    book.start(mine, far, r_far, {"dp_0": 3 - x, "dp_1": 7 - z}, far_from)

    def ring(k, r, step, half):
        if (step, k, r) in r_ring:
            to = wrap(z + step, NZ)
            ref = kv.at[c, wrap(z - step * (k - 1), NZ), r, half]
            pred = received(step, k, r, to) & (x >= r)
            book.start(ref, ref, r_ring[step, k, r] + half, {"dp_1": to}, pred)

    def to_core(ref, at, pred):
        book.start(ref, ref, at, {"dp_2": 1 - c}, pred)

    def ring_start(r):
        for half in (0, 1):
            for s in (1, -1):
                ring(1, r, s, half)

    ring_start(0)
    to_core(mine, r_cx, None)
    for d in (1, 2):
        book.wait(kv.at[c, z, d], r_xk + d - 1, x >= d)
        ring_start(d)
        to_core(kv.at[c, z, d], r_cx + d, x >= d)

    book.wait(qq.at[1 - p], r_q)
    q_pos = (2 * (x * NZ + z) + c) * 256 + lax.broadcasted_iota(jnp.int32, (1, 256), 1)
    q_low, end = jnp.zeros((1, 256), jnp.int32), jnp.int32(0)
    for n in range(lengths.shape[0]):
        end = end + lengths[n]
        q_low = jnp.where(q_pos >= end, end, q_low)

    def attend(zz, row, chunk):
        keys = kv[0, zz, row].reshape(256, HD)
        k_pos = (2 * chunk + p) * 256 + lax.broadcasted_iota(jnp.int32, (256, 256), 0)
        allowed = (k_pos >= q_low) & (k_pos <= q_pos)
        for hd in (0, 1):
            scores = lax.dot_general(keys, qq[hd], (((1,), (1,)), ((), ())), preferred_element_type=F32)
            scores = jnp.where(allowed, scores, LOW)
            old = stat[hd, 0, 0:1]
            new = jnp.maximum(old, jnp.max(scores, axis=0, keepdims=True))
            expw = jnp.where(allowed, jnp.exp(scores - new), 0.0)
            scale = jnp.exp(old - new)
            stat[hd, 1] = stat[hd, 1] * scale + jnp.sum(expw, axis=0, keepdims=True)
            stat[hd, 0] = jnp.broadcast_to(new, (8, 256))
            probs = expw.astype(BF16)
            numer = jnp.dot(kv[1, zz, row, 0], probs[:HD], preferred_element_type=F32)
            numer = numer + jnp.dot(kv[1, zz, row, 1], probs[HD:], preferred_element_type=F32)
            acc[hd] = acc[hd] * scale + numer

    def attend_some(preds, place):
        def one(i, carry):
            on = i < 0
            for n, pred in enumerate(preds):
                if pred is not None:
                    on = on | ((i == n) & pred)

            @pl.when(on)
            def _():
                zz, row = place(i)
                attend(zz, row, (x - row) * NZ + zz)

            return carry

        lax.fori_loop(0, len(preds), one, 0)

    def attend_own():
        for d in (0, 1, 2):
            book.wait(kv.at[1 - c, z, d], r_cx + d, None if d == 0 else x >= d)
        attend_some([x >= 0, x >= 1, x >= 2], lambda i: (z, i))

    def attend_step(k):
        preds = []
        for s in (1, -1):
            for r in range(3):
                need = needed(s, k, r, z)
                if need is not None:
                    need = need & (x >= r)
                    book.wait(kv.at[1 - c, wrap(z - s * k, NZ), r], r_cring[s, k, r], need)
                preds.append(need)
        attend_some(preds, lambda i: (wrap(z - k + 2 * k * lax.div(i, 3), NZ), lax.rem(i, 3)))

    for k in range(1, n_steps + 1):
        for r in range(3):
            steps = [s for s in (1, -1) if (s, k, r) in r_ring]
            for half in (0, 1):
                for s in steps:
                    ref = kv.at[c, wrap(z - s * k, NZ), r, half]
                    book.wait(ref, r_ring[s, k, r] + half, received(s, k, r, z) & (x >= r))
                    ring(k + 1, r, s, half)
            for s in steps:
                to_core(kv.at[c, wrap(z - s * k, NZ), r], r_cring[s, k, r], needed(s, k, r, z) & (x >= r))
        if k == 1:
            book.wait(far, r_far, far_to)
            to_core(far, r_cfar, far_to)
            book.wait(g_o.at[c, z, x], r_o)
            go.x_send()
            attend_own()
        else:
            attend_step(k - 1)
        if k == 3:
            go.x_wait()
        if k == 4:
            go.begin()
    attend_step(4)
    book.wait(kv.at[1 - c, NZ, 0], r_cfar, far_to)

    @pl.when(far_to)
    def _():
        attend(NZ, 0, 7)

    r_acc, r_stat = book.slot(1), book.slot(1)
    o_out[...] = acc[1 - p].astype(BF16)
    book.start(stat.at[1 - p], stat_in, r_stat, {"tp_0": y2})
    book.start(o_out, o_in, r_acc, {"tp_0": y2})
    total[...] = jnp.zeros_like(total)
    book.wait(stat_in, r_stat)
    m_a, m_b = stat[p, 0, 0:1], stat_in[0, 0:1]
    top = jnp.maximum(m_a, m_b)
    e_a, e_b = jnp.exp(m_a - top), jnp.exp(m_b - top)
    denom = stat[p, 1, 0:1] * e_a + stat_in[1, 0:1] * e_b
    book.wait(o_in, r_acc)
    merged = ((acc[p] * e_a + o_in[...].astype(F32) * e_b) / denom).astype(BF16)
    heads[y, h, 0] = merged[:, :HD]
    heads[y, h, 1] = merged[:, HD:]

    r_h = book.slot(2)
    last = ({1: 4, -1: 3}, {1: 3, -1: 4})
    r_head = [{(s, k): book.slot(2) for s in (1, -1) for k in range(1, ends[s] + 1)} for ends in last]
    side = (h, 1 - h)

    def head_hop(which, k, s, half):
        ref = heads.at[wrap(y - s * (k - 1), NY), side[which], half]
        book.start(ref, ref, r_head[which][s, k] + half, {"tp_0": wrap(y + s, NY)})

    def head_step(which, k):
        for half in (0, 1):
            for s in (1, -1):
                if k <= last[which][s]:
                    book.wait(heads.at[wrap(y - s * k, NY), side[which], half], r_head[which][s, k] + half)
                    if k < last[which][s]:
                        head_hop(which, k + 1, s, half)

    for half in (0, 1):
        own = heads.at[y, h, half]
        book.start(own, own, r_h + half, {"tp_1": 1 - h})
        for s in (1, -1):
            head_hop(0, 1, s, half)

    def add_group(yy, hh):
        values = jnp.concatenate([heads[yy, hh, 0], heads[yy, hh, 1]], axis=1)
        term = jnp.dot(w_t[2 * yy + hh], values, preferred_element_type=F32).astype(BF16)
        total[...] = total[...] + term.astype(F32)

    def weights(t, carry):
        yy, hh = lax.div(t, 2), lax.rem(t, 2)
        parts = [g_o[cc, yy, 2 * hh + b].astype(F32) for b in (0, 1) for cc in (0, 1)]
        w_t[t] = jnp.concatenate(parts, axis=0).astype(BF16)
        return carry

    def add_step(which, k):
        steps = [1] if k == 0 else [s for s in (1, -1) if k <= last[which][s]]

        def one(i, carry):
            add_group(wrap(y - k + 2 * k * i, NY) if steps[0] == 1 else wrap(y + k, NY), side[which])
            return carry

        lax.fori_loop(0, len(steps), one, 0)

    go.step(1)
    head_step(0, 1)
    for half in (0, 1):
        book.wait(heads.at[y, 1 - h, half], r_h + half)
        for s in (1, -1):
            head_hop(1, 1, s, half)
    go.step(2)
    head_step(0, 2)
    head_step(1, 1)
    go.step(3)
    head_step(0, 3)
    head_step(1, 2)
    go.step(4)
    head_step(0, 4)
    go.core_wait()
    lax.fori_loop(0, NY * NH, weights, 0)
    add_step(0, 0)
    add_step(1, 0)
    add_step(0, 1)
    add_step(1, 1)
    head_step(1, 3)
    for k in (2, 3):
        add_step(0, k)
    add_step(0, 4)
    for k in (2, 3):
        add_step(1, k)
    head_step(1, 4)
    add_step(1, 4)
    out[...] = total[...].astype(BF16)
    book.finish()


def body(hidden_states, resp_lengths, w_query, w_keyval, w_out):
    rows = hidden_states.shape[0]
    vmem, hbm = pl.BlockSpec(memory_space=pltpu.VMEM), pl.BlockSpec(memory_space=pl.ANY)
    return pl.pallas_call(
        kernel,
        out_shape=jax.ShapeDtypeStruct((224, rows), BF16),
        in_specs=[pl.BlockSpec(memory_space=pltpu.SMEM)] + [hbm] * 4,
        out_specs=vmem,
        scratch_shapes=[
            pltpu.VMEM((256, 3584), BF16),
            pltpu.VMEM((56, 64), BF16),
            pltpu.VMEM((56, HD), BF16),
            pltpu.VMEM((56, HD), BF16),
            pltpu.VMEM((NC, NZ, NX, 56, HD), BF16),
            pltpu.VMEM((NC, NZ, NX, 56, HD), BF16),
            pltpu.VMEM((NC, NZ, NX, 56, HD), BF16),
            pltpu.VMEM((NX, NH, 56, HD), BF16),
            pltpu.VMEM((NX * NZ, 112, HD), BF16),
            pltpu.VMEM((NX * NZ, 112, HD), BF16),
            pltpu.VMEM((16, 224, HD), BF16),
            pltpu.VMEM((2, 256, HD), BF16),
            pltpu.VMEM((2, HD, HD), BF16),
            pltpu.VMEM((2, NZ + 1, 3, 2, HD, HD), BF16),
            pltpu.VMEM((2, HD, 256), F32),
            pltpu.VMEM((2, 2, 8, 256), F32),
            pltpu.VMEM((HD, 256), BF16),
            pltpu.VMEM((HD, 256), BF16),
            pltpu.VMEM((2, 8, 256), F32),
            pltpu.VMEM((NY, NH, 2, HD, HD), BF16),
            pltpu.VMEM((224, 256), F32),
            pltpu.SemaphoreType.DMA((4,)),
            pltpu.SemaphoreType.DMA((40,)),
            pltpu.SemaphoreType.DMA((151,)),
        ],
        compiler_params=pltpu.CompilerParams(
            collective_id=0, has_side_effects=True, vmem_limit_bytes=60 * 1024 * 1024),
        name="layer",
    )(resp_lengths, hidden_states, w_query, w_keyval, w_out.T).T


def solution(mesh):
    finer = Mesh(mesh.devices.reshape(4, 8, 2, 8, 2), (*DP, *TP))
    placed = (P(DP, None), P(), P(DP, TP), P(DP, TP), P(TP, DP))
    return jax.shard_map(body, mesh=finer, in_specs=placed, out_specs=P(DP, TP), check_vma=False)
```

time: 117 us -> 101 us (0.86); the launches traced: 116 us -> 101 us
  Pallas kernels: 110 us -> 99.4 us
  local copies, waits for them, and re-layouts: 3.67 us -> 1.55 us
  other arithmetic: 1.78 us -> 0 us
    pallas_call x1, Pallas kernels: 110 us -> 99.4 us  [body(): pl.pallas_call(kernel, out_shape=jax.ShapeDtypeStruct((224, rows), BF16),...]
    unnamed x6 -> x1, local copies, waits for them, and re-layouts: 2.92 us -> 1.55 us
where the time goes in v2:
time: 101 us
  Pallas kernels  99.4 us (98%)
  local copies, waits for them, and re-layouts  1.55 us (2%)
    pallas_call x1, Pallas kernels, body(): pl.pallas_call(kernel, out_shape=jax.ShapeDtypeStruct((224, rows), BF16),...  99.4 us

profile of v2, /device:TPU:14, one launch (start us, length us, event | category | flops | bytes accessed | tf_op | source)
XLA Modules:
  0.0 100.9 jit_solution(13543925037192935046)
XLA Ops:
  0.0 99.4 %layer.1 = bf16[224,256]{1,0:T(8,128)(2,1)} custom-call(s32[8]{0:T(128)} %lengths.1, bf16[256,3584]{1,0:T(8,128)(2,1)} %hid_in.1, bf16[56,128]{1,0:T(8,128)(2,1)} %wq_in.1, bf16[56,64]{1,0:T(8,128)(2,1)} %wkv_in.1, bf16[56,128]{1,0:T(8,128)(2,1)} %bitcast.3), custom_call_target="tpu_custom_call" | custom-call | tf_op jit(solution)/shard_map/layer/pallas_call | solution.py:516
  99.4 1.6 %copy.7 = bf16[256,224]{0,1:T(8,128)(2,1)} copy(bf16[256,224]{0,1:T(8,128)(2,1)} %bitcast.2) | data formatting | bytes 229376
